TPU v7x, 512 devices: a 4x2x32 block of a 4x8x32 slice. The times are simulated.
512 devices in a mesh: tenant: 2 (over y), ctx: 32 (over z), head: 8 (over x, core).
Axes of the slice: x: 4, y: 2, z: 32, core: 2. Of those that a mesh axis runs over, the one named last changes fastest.
The devices are a block of a 4x8x32 slice.
Arguments:
- tokens: bfloat16 [16384, 4608], P(('tenant', 'ctx'), 'head'), parts along dimension 0, may hold values from -6 to 6
- query_frozen_matrix: bfloat16 [4608, 2048], P('ctx', 'head'), may hold values from -0.09375 to 0.09375
- key_weight: bfloat16 [4608, 1024], P('ctx', 'head'), may hold values from -0.09375 to 0.09375
- value_frozen_matrix: bfloat16 [4608, 1024], P('ctx', 'head'), may hold values from -0.09375 to 0.09375
- query_down: bfloat16 [9216, 16], P('tenant'), parts along dimension 0, may hold values from -0.09375 to 0.09375
- query_adapter_expand: bfloat16 [32, 2048], P('tenant', 'head'), parts along dimension 0, may hold values from -1.5 to 1.5
- value_down: bfloat16 [9216, 16], P('tenant'), parts along dimension 0, may hold values from -0.09375 to 0.09375
- value_adapter_expand: bfloat16 [32, 1024], P('tenant', 'head'), parts along dimension 0, may hold values from -1.5 to 1.5
- block_order: int32 [128], P('tenant'), parts along dimension 0, may hold values from 0 to 63, each once
- doc_starts: int32 [24], P('tenant'), parts along dimension 0, may hold values from 0 to 8191, as said below
- prompt_of: int32 [24], P('tenant'), parts along dimension 0, may hold values from 0 to 11, as said below
Outputs:
- attended: bfloat16 [16384, 2048], P(('tenant', 'ctx'), 'head'), parts along dimension 0
There are 2 independent parts, one for each index of `tenant`. A program takes and returns all parts, laid end to end along the dimension named above; an argument that names none is the same for every part. Nothing has to cross between parts.
Inputs may be any that keep to these rules, and one draw needn't show every extreme that they name: `doc_starts`: strictly increasing with first entry 0; the segments come in 4 groups of three: a prompt, a chosen and a rejected response. `prompt_of`: for segment j = 3k it is j; for j = 3k + 1 it is 3k; for j = 3k + 2 it is 3k or j. `block_order`: each of 0 to 63 once.
All inputs are finite; a program needn't handle non-finite values.
Results may differ from a plain program's by a relative error of at most 0.012.
Values may be sent and summed in bfloat16 or wider, within the bound.
A program may use at most 64 MiB of HBM per device.

v0:
```python
import math

import jax
import jax.numpy as jnp
from jax import lax
from jax.sharding import PartitionSpec as P

HD = 128


softcap_limit = 50.0
query_scale = 144.0 ** (-0.5)
adapter_scaling = 2.0
rope_base = 10000.0


def from_everyone(x, axis):
    copies = jnp.broadcast_to(x, (lax.axis_size(axis), *x.shape))
    return lax.all_to_all(copies, axis, split_axis=0, concat_axis=0, tiled=True)


def joined_along(pieces, dim):
    dims = list(pieces.shape[1:])
    dims[dim] *= pieces.shape[0]
    return jnp.moveaxis(pieces, 0, dim).reshape(dims)


def gather_directly(x, axis, dim):
    pieces = from_everyone(x, axis)
    return joined_along(pieces, dim)


def sent_together(arrays, axis, dim, along):
    widths = [a.shape[along] for a in arrays]
    both = jnp.concatenate(arrays, axis=along)
    whole = lax.all_gather(both, axis, axis=dim, tiled=True)
    return tuple(jnp.split(whole, [sum(widths[:k]) for k in range(1, len(widths))], axis=along))


def row_meta(row_ids, block_order, doc_starts, prompt_of, block_len, sequence_len):
    block_count = block_order.shape[0]
    block_id = row_ids // block_len
    one_hot = block_id[:, None] == jnp.arange(block_count, dtype=jnp.int32)[None, :]
    ordered = jnp.sum(jnp.where(one_hot, block_order[None, :], 0), axis=1)
    places = ordered * block_len + row_ids % block_len
    segment = jnp.sum((doc_starts[None, :] <= places[:, None]).astype(jnp.int32), axis=1) - 1
    seg_ids = jnp.arange(doc_starts.shape[0], dtype=jnp.int32)
    selected = segment[:, None] == seg_ids[None, :]
    prompt_seg = jnp.sum(jnp.where(selected, prompt_of[None, :], 0), axis=1)
    own_start = jnp.sum(jnp.where(selected, doc_starts[None, :], 0), axis=1)
    next_starts = jnp.concatenate([doc_starts[1:], jnp.full((1,), sequence_len, jnp.int32)])
    prompt_sel = prompt_seg[:, None] == seg_ids[None, :]
    prompt_len = jnp.sum(jnp.where(prompt_sel, (next_starts - doc_starts)[None, :], 0), axis=1)
    rotary_pos = places - own_start + jnp.where(prompt_seg != segment, prompt_len, 0)
    return (places, segment, prompt_seg, rotary_pos)


def rotate(values_in, rotary_pos):
    width_half = values_in.shape[-1] // 2
    frequency = jnp.exp(
        jnp.arange(width_half, dtype=jnp.float32)
        * (-2.0 * math.log(rope_base) / values_in.shape[-1])
    )
    angles = rotary_pos.astype(jnp.float32)[:, None] * frequency[None, :]
    cosine = jnp.concatenate([jnp.cos(angles), jnp.cos(angles)], axis=-1)[:, None, :]
    sine_part = jnp.concatenate([jnp.sin(angles), jnp.sin(angles)], axis=-1)[:, None, :]
    rotated = jnp.concatenate([-values_in[..., width_half:], values_in[..., :width_half]], axis=-1)
    return values_in * cosine + rotated * sine_part


def visible_mask(query_info, key_info):
    same_doc = (key_info[1][None, :] == query_info[1][:, None]) & (
        key_info[0][None, :] <= query_info[0][:, None]
    )
    from_prompt = (key_info[1][None, :] == query_info[2][:, None]) & (
        query_info[2] != query_info[1]
    )[:, None]
    return same_doc | from_prompt


def local(
    tokens,
    query_frozen_matrix,
    key_weight,
    value_frozen_matrix,
    query_down,
    query_adapter_expand,
    value_down,
    value_adapter_expand,
    block_order,
    doc_starts,
    prompt_of,
):
    tok_rows = tokens.shape[0]
    cycle_size = lax.axis_size("ctx")
    device = lax.axis_index("ctx")
    sequence_len = tok_rows * cycle_size
    block_len = tok_rows // 2
    full_tokens = gather_directly(tokens, "head", 1)

    def add_rows(weight_part):
        return jnp.dot(full_tokens, weight_part, preferred_element_type=jnp.float32)

    pieces = sent_together((query_frozen_matrix, key_weight, value_frozen_matrix), "ctx", 0, 1)
    frozen_query_output = add_rows(pieces[0])
    key_base = add_rows(pieces[1])
    frozen_value_output = add_rows(pieces[2])
    own_ids = device * tok_rows + jnp.arange(tok_rows, dtype=jnp.int32)
    own_info = row_meta(own_ids, block_order, doc_starts, prompt_of, block_len, sequence_len)
    local_heads = query_frozen_matrix.shape[1] // HD
    local_kv = key_weight.shape[1] // HD
    per_kv = local_heads // local_kv
    query_adapter_hidden = jnp.dot(
        full_tokens, query_down, preferred_element_type=jnp.float32
    ).astype(jnp.bfloat16)
    query_states = frozen_query_output + adapter_scaling * jnp.dot(
        query_adapter_hidden, query_adapter_expand, preferred_element_type=jnp.float32
    )
    query_states = (
        rotate(query_states.reshape(tok_rows, local_heads, HD), own_info[3]) * query_scale
    ).astype(jnp.bfloat16)
    query_heads = query_states.reshape(tok_rows, local_kv, per_kv, HD)
    key_proj = (
        rotate(key_base.reshape(tok_rows, local_kv, HD), own_info[3])
        .astype(jnp.bfloat16)
        .reshape(tok_rows, local_kv * HD)
    )
    value_adapter_hidden = jnp.dot(
        full_tokens, value_down, preferred_element_type=jnp.float32
    ).astype(jnp.bfloat16)
    value_projected = (
        frozen_value_output
        + adapter_scaling
        * jnp.dot(value_adapter_hidden, value_adapter_expand, preferred_element_type=jnp.float32)
    ).astype(jnp.bfloat16)
    pieces = sent_together((key_proj, value_projected), "ctx", 0, 1)
    key_ids = jnp.arange(pieces[0].shape[0], dtype=jnp.int32)
    key_block = pieces[0]
    value_block = pieces[1]
    key_info = row_meta(key_ids, block_order, doc_starts, prompt_of, block_len, sequence_len)
    visible = visible_mask(own_info, key_info)
    key_heads = key_block.reshape(key_block.shape[0], local_kv, HD)
    value_heads = value_block.reshape(value_block.shape[0], local_kv, HD)
    scores = jnp.einsum(
        "tkgd,skd->kgts", query_heads, key_heads, preferred_element_type=jnp.float32
    )
    capped = softcap_limit * jnp.tanh(scores / softcap_limit)
    unnorm = jnp.where(visible[None, None], jnp.exp(capped), jnp.zeros_like(capped))
    denominator = jnp.sum(unnorm, axis=-1)
    numerator = jnp.einsum(
        "kgts,skd->tkgd",
        unnorm.astype(jnp.bfloat16),
        value_heads,
        preferred_element_type=jnp.float32,
    )
    numerator, denominator = (numerator, denominator)
    attended = numerator / jnp.transpose(denominator, (2, 0, 1))[..., None]
    return attended.reshape(tok_rows, local_heads * HD).astype(jnp.bfloat16)


def solution(mesh):
    in_specs = (
        P(("tenant", "ctx"), "head"),
        P("ctx", "head"),
        P("ctx", "head"),
        P("ctx", "head"),
        P("tenant", None),
        P("tenant", "head"),
        P("tenant", None),
        P("tenant", "head"),
        P("tenant"),
        P("tenant"),
        P("tenant"),
    )
    out_specs = P(("tenant", "ctx"), "head")
    return jax.shard_map(local, mesh=mesh, in_specs=in_specs, out_specs=out_specs, check_vma=False)
```

profile of v0, /device:TPU:40, one launch (start us, length us, event | category | flops | bytes accessed | tf_op | source)
XLA Modules:
  0.0 342.5 jit_solution(15707848567135938474)
XLA Ops:
  6.5 0.0 copy-start
  6.6 0.0 all-gather.3.cloned.1.call-start
  6.6 1.6 pad_maximum_fusion
  8.2 0.1 all-gather.3.cloned.1.call-update
  8.3 2.6 broadcast_in_dim.57
  10.8 0.0 copy-start.3
  10.8 0.0 copy-start.5
  10.8 0.0 copy-start.6
  10.8 0.0 copy-start.1
  10.8 0.0 copy-start.4
  10.8 4.7 %all-to-all-start = ((bf16[8,256,576]{1,2,0:T(8,128)(2,1)}), bf16[8,256,576]{1,2,0:T(8,128)(2,1)S(1)}, u32[]{:S(2)}, u32[]{:S(2)}) async-start(bf16[8,256,576]{1,2,0:T(8,128)(2,1)} %broadcast_in_dim.57), calls=%async_computation | async-start | bytes 4718592 | tf_op jit(solution)/shard_map/all_to_all | solution.py:19
  15.6 0.1 all-gather.5.cloned.1.call-start
  15.6 0.0 copy-done.3
  15.6 0.1 slice.15
  15.7 0.0 copy-done.5
  15.8 0.1 select_reduce_fusion.1
  15.9 0.1 convert_reduce_fusion.1
  16.0 0.0 copy-done.6
  16.0 0.1 select_reduce_fusion.4
  16.1 0.1 add_subtract_fusion
  16.1 0.1 select_reduce_fusion.2
  16.2 0.3 multiply_cosine_fusion
  16.5 29.0 %all-to-all-done = bf16[8,256,576]{1,2,0:T(8,128)(2,1)S(1)} async-done(((bf16[8,256,576]{1,2,0:T(8,128)(2,1)}), bf16[8,256,576]{1,2,0:T(8,128)(2,1)S(1)}, u32[]{:S(2)}, u32[]{:S(2)}) %all-to-all-start) | async-done | bytes 2359328 | tf_op jit(solution)/shard_map/all_to_all | solution.py:19
  45.5 0.0 copy-done.1
  45.5 0.0 copy-done.4
  45.5 0.6 convolution_multiply_fusion.1
  46.2 129.8 %all-gather.3.cloned.1.call-done = bf16[4608,512]{1,0:T(8,128)(2,1)} async-done(((bf16[144,512]{1,0:T(8,128)(2,1)}), bf16[4608,512]{1,0:T(8,128)(2,1)}) %all-gather.3.cloned.1.call-update) | async-done | bytes 4718608 | tf_op jit(solution)/shard_map/all_gather | solution.py:36
  175.9 1.8 fusion.7
  177.8 1.9 fusion.30
  179.7 0.0 copy-start.2
  179.8 0.7 pad_maximum_fusion.3
  180.4 0.1 all-gather.5.cloned.1.call-update
  180.5 0.4 select_reduce_fusion
  180.9 0.2 convert_reduce_fusion
  181.1 6.4 %and_or_fusion = pred[256,8192]{0,1:T(8,128)(4,1)} fusion(s32[256]{0:T(256)S(1)} %get-tuple-element.6, s32[256]{0:T(256)S(1)} %fusion.46, s32[256]{0:T(256)S(1)} %broadcast_add_fusion.1, s32[8192]{0:T(1024)S(1)} %fusion.44, s32[8192]{0:T(1024)S(1)} %broadcast_add_fusion, pred[256]{0:T(512)(128)(4,1)S(1)} %get-tuple-element.8), kind=kLoop, calls=%fused_computation.4 | loop fusion | flops 12582912 | bytes 2166016 | tf_op jit(solution)/shard_map/or | solution.py:78
  187.5 0.0 copy-done
  187.5 0.0 copy-done.2
  187.5 0.6 convolution_multiply_fusion
  188.2 2.5 fusion.12
  190.8 135.0 %all-gather.5.cloned.1.call-done = bf16[8192,256]{0,1:T(8,128)(2,1)} async-done(((bf16[256,256]{0,1:T(8,128)(2,1)}), bf16[8192,256]{0,1:T(8,128)(2,1)}) %all-gather.5.cloned.1.call-update) | async-done | bytes 4194320 | tf_op jit(solution)/shard_map/all_gather | solution.py:36
  325.8 0.0 copy-start.7
  325.8 7.8 %fusion.50 = (f32[2,256]{1,0:T(2,128)S(1)}, bf16[1,2,256,8192]{2,3,1,0:T(8,128)(2,1)S(1)}) fusion(bf16[256,2,128]{0,2,1:T(8,128)(2,1)S(1)} %bitcast.94, bf16[8192,256]{0,1:T(8,128)(2,1)} %all-gather.5.cloned.1.call-done, pred[256,8192]{0,1:T(8,128)(4,1)} %and_or_fusion), kind=kOutput, calls=%fused_computation.82 | convolution fusion | flops 1094712832 | bytes 12716032 | tf_op jit(solution)/shard_map/tkgd,skd->kgts/dot_general | solution.py:144
  333.6 0.0 copy-done.7
  333.6 1.3 fusion.21
  334.9 0.8 copy.24
  (13 shorter events, 0.2 us)
Async XLA Ops:
  6.5 181.0 %copy-start = (bf16[4608,16]{0,1:T(8,128)(2,1)S(1)}, bf16[4608,16]{0,1:T(8,128)(2,1)}, u32[]{:S(2)}) copy-start(bf16[4608,16]{0,1:T(8,128)(2,1)} %param.15) | copy-start | bytes 442372
  6.6 169.4 %all-gather.3.cloned.1.call-start = ((), (), s32[]{:S(2)}) async-start(), calls=%async_computation.1 | async-start | bytes 4866048 | tf_op jit(solution)/shard_map/all_gather | solution.py:36
  10.8 4.8 %copy-start.3 = (s32[12]{0:T(128)S(1)}, s32[12]{0:T(128)}, u32[]{:S(2)}) copy-start(s32[12]{0:T(128)} %param.20) | copy-start | bytes 148
  10.8 4.9 %copy-start.5 = (s32[64]{0:T(128)S(1)}, s32[64]{0:T(128)}, u32[]{:S(2)}) copy-start(s32[64]{0:T(128)} %param.19) | copy-start | bytes 772
  10.8 5.1 %copy-start.6 = (s32[12]{0:T(128)S(1)}, s32[12]{0:T(128)}, u32[]{:S(2)}) copy-start(s32[12]{0:T(128)} %param.21) | copy-start | bytes 148
  10.8 34.7 %copy-start.1 = (bf16[4608,16]{0,1:T(8,128)(2,1)S(1)}, bf16[4608,16]{0,1:T(8,128)(2,1)}, u32[]{:S(2)}) copy-start(bf16[4608,16]{0,1:T(8,128)(2,1)} %param.17) | copy-start | bytes 442372
  10.8 34.7 %copy-start.4 = (bf16[16,128]{1,0:T(8,128)(2,1)S(1)}, bf16[16,128]{1,0:T(8,128)(2,1)}, u32[]{:S(2)}) copy-start(bf16[16,128]{1,0:T(8,128)(2,1)} %param.18) | copy-start | bytes 12292
  10.8 34.7 %all-to-all-start = ((bf16[8,256,576]{1,2,0:T(8,128)(2,1)}), bf16[8,256,576]{1,2,0:T(8,128)(2,1)S(1)}, u32[]{:S(2)}, u32[]{:S(2)}) async-start(bf16[8,256,576]{1,2,0:T(8,128)(2,1)} %broadcast_in_dim.57), calls=%async_computation | async-start | bytes 4718592 | tf_op jit(solution)/shard_map/all_to_all | solution.py:19
  15.6 310.2 %all-gather.5.cloned.1.call-start = ((), (), s32[]{:S(2)}) async-start(), calls=%async_computation.2 | async-start | bytes 4325376 | tf_op jit(solution)/shard_map/all_gather | solution.py:36
  179.7 7.8 %copy-start.2 = (bf16[16,256]{1,0:T(8,128)(2,1)S(1)}, bf16[16,256]{1,0:T(8,128)(2,1)}, u32[]{:S(2)}) copy-start(bf16[16,256]{1,0:T(8,128)(2,1)} %param.16) | copy-start | bytes 24580
  325.8 7.8 %copy-start.7 = (bf16[8192,256]{0,1:T(8,128)(2,1)S(1)}, bf16[8192,256]{0,1:T(8,128)(2,1)}, u32[]{:S(2)}) copy-start(bf16[8192,256]{0,1:T(8,128)(2,1)} %all-gather.5.cloned.1.call-done) | copy-start | bytes 12582916
Sparse Core Ops, SparseCore 0:
  9.4 166.4 all-gather.2
  180.6 145.0 all-gather.4
where the time goes:
time: 343 us; the launch traced here: 342 us
  waiting for transfers between devices  294 us (86%)
  matrix products  16.5 us (5%)
  between operations  13.6 us (4%)
  other arithmetic  10.3 us (3%)
  starting transfers between devices  4.79 us (1%)
  local copies, waits for them, and re-layouts  3.43 us (1%)
    all_gather x2, waiting for transfers between devices, sent_together(): whole = lax.all_gather(both, axis, axis=dim, tiled=True)  265 us
    all_to_all x1, waiting for transfers between devices, from_everyone(): return lax.all_to_all(copies, axis, split_axis=0, concat_axis=0, tiled=True)  29 us
    dot_general x1, matrix products, local(): jnp.einsum('tkgd,skd->kgts', query_heads, key_heads, preferred_element_ty...  7.82 us
  transfers between devices with their start and end apart: 3, of which 3 were waited for; matrix products, arithmetic and copies ran while one was open for 4% of the time, Pallas kernels for 0%

commit v1 on v0

v1 whole, which is shorter than its diff:
```python
import functools
import math

import jax
import jax.numpy as jnp
from jax import lax
from jax.experimental import pallas as pl
from jax.experimental.pallas import tpu as pltpu
from jax.sharding import PartitionSpec as P

HD = 128
MESH = pl.DeviceIdType.MESH
softcap_limit = 50.0
query_scale = 144.0 ** (-0.5)
adapter_scaling = 2.0
rope_base = 10000.0
exp_scale = softcap_limit / math.log(2.0)


def dot(a, b):
    return jnp.dot(a, b, preferred_element_type=jnp.float32)


def dot_nt(a, b):
    return lax.dot_general(a, b, (((1,), (1,)), ((), ())), preferred_element_type=jnp.float32)


def kernel(
    n, heads, freq_ref, tok_ref, wq_ref, wk_ref, wv_ref, qd_ref, qe_ref, vd_ref, ve_ref,
    order_ref, starts_ref, prompt_ref, out_ref,
    tok_all, w_all, kv_all, low_q, low_v, acc_kv, acc_q, q_s, geo, cos_s, sin_s, num, den,
    t_send, t_recv, d_send, d_recv, w_send, w_recv, k_send, k_recv,
):
    me = lax.axis_index("ctx")
    head = lax.axis_index("head")
    rows, feat = tok_ref.shape
    depth = wq_ref.shape[0]
    half_steps = n // 2
    group = feat // depth
    chips = heads // 2
    segs = starts_ref.shape[0]
    block_len = rows // 2
    right = lax.rem(me + 1, n)
    left = lax.rem(me + n - 1, n)
    partner = head + 1 - 2 * lax.rem(head, 2)

    def same_core(step):
        return lax.rem(head + 2 * step, heads)

    barrier = pltpu.get_barrier_semaphore()
    for ctx in (left, right):
        pl.semaphore_signal(barrier, inc=1, device_id={"ctx": ctx}, device_id_type=MESH)
    pl.semaphore_signal(barrier, inc=1, device_id={"head": partner}, device_id_type=MESH)
    for k in range(1, chips):
        pl.semaphore_signal(barrier, inc=1, device_id={"head": same_core(k)}, device_id_type=MESH)
    pl.semaphore_wait(barrier, 3 + chips - 1)

    def weight_source(c):
        if c == 0:
            return wk_ref
        if c == 1:
            return wv_ref
        return wq_ref.at[:, pl.ds((c - 2) * HD, HD)]

    def block_at(d, step):
        return lax.rem(me + step, n) if d else lax.rem(me + n - step, n)

    def w_slot(c, block):
        return w_all.at[c, pl.ds(pl.multiple_of(block * depth, depth), depth)]

    def w_copy(d, step, c):
        block = block_at(d, step - 1)
        return pltpu.make_async_remote_copy(
            src_ref=weight_source(c) if step == 1 else w_slot(c, block),
            dst_ref=w_slot(c, block),
            send_sem=w_send.at[d, step - 1, c],
            recv_sem=w_recv.at[d, step - 1, c],
            device_id={"ctx": left if d else right},
            device_id_type=MESH,
        )

    def w_wait(d, step, c):
        slot = w_slot(c, block_at(d, step))
        pltpu.make_async_remote_copy(
            src_ref=slot, dst_ref=slot, send_sem=w_send.at[d, step - 1, c],
            recv_sem=w_recv.at[d, step - 1, c], device_id={"ctx": right}, device_id_type=MESH,
        ).wait_recv()

    def w_ways(step):
        if step < half_steps:
            return [(d, c) for c in range(4) for d in range(2)]
        return [(0, 0), (1, 2), (0, 1), (1, 3)]

    for d, c in w_ways(1):
        w_copy(d, 1, c).start()

    def t_copy(k):
        return pltpu.make_async_remote_copy(
            src_ref=tok_ref, dst_ref=tok_all.at[head], send_sem=t_send.at[k], recv_sem=t_recv.at[k],
            device_id={"head": same_core(k)}, device_id_type=MESH,
        )

    def t_wait(k):
        slot = tok_all.at[lax.rem(head + heads - 2 * k, heads)]
        pltpu.make_async_remote_copy(
            src_ref=slot, dst_ref=slot, send_sem=t_send.at[k], recv_sem=t_recv.at[k],
            device_id={"head": partner}, device_id_type=MESH,
        ).wait_recv()

    def d_copy(k):
        source = lax.rem(head + heads - 2 * k, heads)
        return pltpu.make_async_remote_copy(
            src_ref=tok_ref if k == 0 else tok_all.at[source], dst_ref=tok_all.at[source],
            send_sem=d_send.at[k], recv_sem=d_recv.at[k],
            device_id={"head": partner}, device_id_type=MESH,
        )

    def d_wait(k):
        slot = tok_all.at[lax.rem(partner + heads - 2 * k, heads)]
        pltpu.make_async_remote_copy(
            src_ref=slot, dst_ref=slot, send_sem=d_send.at[k], recv_sem=d_recv.at[k],
            device_id={"head": partner}, device_id_type=MESH,
        ).wait_recv()

    for k in range(1, chips):
        t_copy(k).start()
    d_copy(0).start()

    tok_all[head] = tok_ref[...]
    own = pl.ds(pl.multiple_of(me * depth, depth), depth)
    w_all[0, own] = wk_ref[...]
    w_all[1, own] = wv_ref[...]
    w_all[2, own] = wq_ref[:, :HD]
    w_all[3, own] = wq_ref[:, HD:]

    sequence_len = rows * n

    def geometry():
        place = lax.broadcasted_iota(jnp.int32, (block_len, HD), 0)
        for part in range(2):
            p = place + order_ref[2 * me + part] * block_len
            a = jnp.zeros_like(p)
            b = jnp.zeros_like(p)
            e = jnp.zeros_like(p)
            for j in range(segs):
                m = prompt_ref[j]
                reads = m != j
                stop = jnp.where(m + 1 < segs, starts_ref[jnp.minimum(m + 1, segs - 1)], sequence_len)
                begin = jnp.where(reads, starts_ref[m], 0)
                stop = jnp.where(reads, stop, 0)
                start = starts_ref[j]
                here = p >= start
                a = jnp.where(here, start, a)
                b = jnp.where(here, begin, b)
                e = jnp.where(here, stop, e)
            span = pl.ds(part * block_len, block_len)
            geo[0, span] = a
            geo[1, span] = p
            geo[2, span] = b
            geo[3, span] = e
            angle = (p - a + e - b).astype(jnp.float32) * freq_ref[...]
            lane = lax.broadcasted_iota(jnp.int32, (block_len, HD), 1)
            sine = jnp.sin(angle)
            cos_s[span] = jnp.cos(angle)
            sin_s[span] = jnp.where(lane < HD // 2, -sine, sine)

    def add_group(g, first=False):
        tok = tok_all[g]
        span = pl.ds(pl.multiple_of(g * feat, feat), feat)
        kv = dot(tok, jnp.concatenate([w_all[0, span], w_all[1, span]], axis=1))
        q = dot(tok, jnp.concatenate([w_all[2, span], w_all[3, span]], axis=1))
        if first:
            acc_kv[...] = kv
            acc_q[...] = q
        else:
            acc_kv[...] += kv
            acc_q[...] += q

    def add_low(h):
        span = pl.ds(h * feat, feat)
        tok = tok_all[h]
        q = dot_nt(tok, qd_ref[:, span])
        v = dot_nt(tok, vd_ref[:, span])
        if h == 0:
            low_q[...] = q
            low_v[...] = v
        else:
            low_q[...] += q
            low_v[...] += v

    forward_at = half_steps * 6 // 16
    arrive_at = half_steps * 9 // 16
    waiting = {}
    my_group = me // group
    for j in range(heads // 2 + 1):
        ready = min(group * j + group - 1, half_steps)
        gs = [my_group] if j == 0 else [lax.rem(my_group + j, heads)]
        if 0 < j < heads // 2:
            gs.append(lax.rem(my_group + heads - j, heads))
        for g in gs:
            waiting.setdefault(max(ready, arrive_at), []).append(g)
    queue = []
    low_left = list(range(heads))
    first = True
    for step in range(1, half_steps + 1):
        for d, c in w_ways(step):
            w_wait(d, step, c)
            if step < half_steps and (d, c) in w_ways(step + 1):
                w_copy(d, step + 1, c).start()
        if step == 1:
            geometry()
        if step == forward_at:
            for k in range(1, chips):
                t_wait(k)
                d_copy(k).start()
        if step == arrive_at:
            for k in range(chips):
                d_wait(k)
        queue += waiting.get(step, [])
        take = len(queue) if step == half_steps else 1
        for g in queue[:take]:
            add_group(g, first)
            first = False
        queue = queue[take:]
        if step > arrive_at:
            take = 2 if step < half_steps - 1 else len(low_left)
            for h in low_left[:take]:
                add_low(h)
            low_left = low_left[take:]

    def k_slot(c, block):
        return kv_all.at[c, pl.ds(pl.multiple_of(block * rows, rows), rows)]

    def rotated(x):
        return x * cos_s[...] + pltpu.roll(x, HD // 2, 1) * sin_s[...]

    own_rows = pl.ds(pl.multiple_of(me * rows, rows), rows)
    kv_all[0, own_rows] = rotated(acc_kv[:, :HD]).astype(jnp.bfloat16)
    low = low_v[...].astype(jnp.bfloat16)
    kv_all[1, own_rows] = (acc_kv[:, HD:] + adapter_scaling * dot(low, ve_ref[...])).astype(jnp.bfloat16)
    low = low_q[...].astype(jnp.bfloat16)
    q = acc_q[...] + adapter_scaling * dot(low, qe_ref[...])
    for i in range(2):
        q_s[i] = (rotated(q[:, i * HD:(i + 1) * HD]) * query_scale).astype(jnp.bfloat16)

    def k_copy(d, step, c):
        block = block_at(d, step - 1)
        slot = k_slot(c, block)
        return pltpu.make_async_remote_copy(
            src_ref=slot, dst_ref=slot,
            send_sem=k_send.at[d, step - 1, c], recv_sem=k_recv.at[d, step - 1, c],
            device_id={"ctx": left if d else right}, device_id_type=MESH,
        )

    def k_wait(d, step, c):
        slot = k_slot(c, block_at(d, step))
        pltpu.make_async_remote_copy(
            src_ref=slot, dst_ref=slot, send_sem=k_send.at[d, step - 1, c],
            recv_sem=k_recv.at[d, step - 1, c], device_id={"ctx": right}, device_id_type=MESH,
        ).wait_recv()

    for c in range(2):
        for d in range(2):
            k_copy(d, 1, c).start()

    def attend(block, first=False):
        span = pl.ds(pl.multiple_of(block * rows, rows), rows)
        keys = kv_all[0, span]
        values = kv_all[1, span]
        lane = lax.broadcasted_iota(jnp.int32, (8, block_len), 1)
        places = [lane + order_ref[2 * block + part] * block_len for part in range(2)]
        tile = block_len
        for t in range(2):
            r = pl.ds(t * tile, tile)
            a, p, b, e = (geo[k, r].reshape(tile // 8, 8, HD) for k in range(4))
            visible = []
            for place in places:
                c = place[None]
                seen = ((c >= a) & (c <= p)) | ((c >= b) & (c < e))
                visible.append(seen.reshape(tile, HD))
            for i in range(2):
                s = dot_nt(q_s[i, r], keys)
                w = jnp.exp2(jnp.tanh(s * (1.0 / softcap_limit)) * exp_scale)
                w0 = jnp.where(visible[0], w[:, :HD], 0.0)
                w1 = jnp.where(visible[1], w[:, HD:], 0.0)
                total = dot(jnp.concatenate([w0.astype(jnp.bfloat16), w1.astype(jnp.bfloat16)], axis=1), values)
                if first:
                    den[i, r] = w0 + w1
                    num[i, r] = total
                else:
                    den[i, r] += w0 + w1
                    num[i, r] += total

    attend(me, True)

    def k_step(step, carry):
        for c in range(2):
            for d in range(2):
                k_wait(d, step, c)
                k_copy(d, step + 1, c).start()
        attend(block_at(0, step))
        attend(block_at(1, step))
        return carry

    lax.fori_loop(1, half_steps - 1, k_step, 0)
    step = half_steps - 1
    for c in range(2):
        for d in range(2):
            k_wait(d, step, c)
            if c == d:
                k_copy(d, step + 1, c).start()
    attend(block_at(0, step))
    attend(block_at(1, step))
    for c in range(2):
        k_wait(c, half_steps, c)
    attend(block_at(0, half_steps))

    for i in range(2):
        total = jnp.sum(den[i], axis=1, keepdims=True)
        out_ref[:, i * HD:(i + 1) * HD] = (num[i] / total).astype(jnp.bfloat16)

    for k in range(1, chips):
        t_copy(k).wait_send()
    for k in range(chips):
        d_copy(k).wait_send()
    for step in range(1, half_steps + 1):
        for d, c in w_ways(step):
            w_copy(d, step, c).wait_send()

    def k_sent(step, carry):
        for c in range(2):
            for d in range(2):
                k_copy(d, step, c).wait_send()
        return carry

    lax.fori_loop(1, half_steps, k_sent, 0)
    for c in range(2):
        k_copy(c, half_steps, c).wait_send()


def local(n, heads, tokens, wq, wk, wv, qd, qe, vd, ve, order, starts, prompts):
    rows, feat = tokens.shape
    depth = wq.shape[0]
    half = HD // 2
    lanes = jnp.arange(half, dtype=jnp.float32)
    freq = jnp.exp(lanes * (-2.0 * math.log(rope_base) / HD))
    freq = jnp.concatenate([freq, freq])[None, :]
    vmem = pl.BlockSpec(memory_space=pltpu.VMEM)
    smem = pl.BlockSpec(memory_space=pltpu.SMEM)
    bf16, f32 = jnp.bfloat16, jnp.float32
    dma = pltpu.SemaphoreType.DMA
    steps = n // 2
    return pl.pallas_call(
        functools.partial(kernel, n, heads),
        out_shape=jax.ShapeDtypeStruct((rows, wq.shape[1]), bf16),
        in_specs=[vmem] * 9 + [smem] * 3,
        out_specs=vmem,
        scratch_shapes=[
            pltpu.VMEM((heads, rows, feat), bf16),
            pltpu.VMEM((4, n * depth, HD), bf16),
            pltpu.VMEM((2, n * rows, HD), bf16),
            pltpu.VMEM((rows, qd.shape[1]), f32),
            pltpu.VMEM((rows, vd.shape[1]), f32),
            pltpu.VMEM((rows, 2 * HD), f32),
            pltpu.VMEM((rows, 2 * HD), f32),
            pltpu.VMEM((2, rows, HD), bf16),
            pltpu.VMEM((4, rows, HD), jnp.int32),
            pltpu.VMEM((rows, HD), f32),
            pltpu.VMEM((rows, HD), f32),
            pltpu.VMEM((2, rows, HD), f32),
            pltpu.VMEM((2, rows, HD), f32),
            dma((heads // 2,)), dma((heads // 2,)), dma((heads // 2,)), dma((heads // 2,)),
            dma((2, steps, 4)), dma((2, steps, 4)),
            dma((2, steps, 2)), dma((2, steps, 2)),
        ],
        compiler_params=pltpu.CompilerParams(
            collective_id=0, has_side_effects=True, vmem_limit_bytes=48 * 1024 * 1024
        ),
    )(freq, tokens, wq, wk, wv, qd.T, qe, vd.T, ve, order, starts, prompts)


def solution(mesh):
    n, heads = mesh.shape["ctx"], mesh.shape["head"]
    in_specs = (
        P(("tenant", "ctx"), "head"),
        P("ctx", "head"),
        P("ctx", "head"),
        P("ctx", "head"),
        P("tenant", None),
        P("tenant", "head"),
        P("tenant", None),
        P("tenant", "head"),
        P("tenant"),
        P("tenant"),
        P("tenant"),
    )
    out_specs = P(("tenant", "ctx"), "head")
    return jax.shard_map(
        functools.partial(local, n, heads), mesh=mesh, in_specs=in_specs, out_specs=out_specs, check_vma=False
    )
```

time: 343 us -> 173 us (0.50)
  waiting for transfers between devices: 294 us -> 0 us
  Pallas kernels: 0 us -> 171 us
  matrix products: 16.5 us -> 0 us
  between operations: 13.6 us -> 0.15 us
  other arithmetic: 10.3 us -> 0.09 us
  starting transfers between devices: 4.79 us -> 0 us
    all_gather x2 -> x0, waiting for transfers between devices: 265 us -> none  [sent_together(): whole = lax.all_gather(both, axis, axis=dim, tiled=True)]
    pallas_call x0 -> x1, Pallas kernels: none -> 171 us  [local(): pl.pallas_call(functools.partial(kernel, n, heads), out_shape=jax.ShapeDt...]
    all_to_all x1 -> x0, waiting for transfers between devices: 29 us -> none  [from_everyone(): return lax.all_to_all(copies, axis, split_axis=0, concat_axis=0, tiled=True)]
    dot_general x7 -> x0, matrix products: 16.5 us -> none  [the longest x1 7.82 us: local(): jnp.einsum('tkgd,skd->kgts', query_heads, key_heads, preferred_element_ty...]
    or x1 -> x0, other arithmetic: 6.42 us -> none  [visible_mask(): return same_doc | from_prompt]
    all_to_all x1 -> x0, starting transfers between devices: 4.73 us -> none  [from_everyone(): return lax.all_to_all(copies, axis, split_axis=0, concat_axis=0, tiled=True)]
  transfers between devices with their start and end apart: 3 -> 0, of which waited for: 3 -> 0; matrix products, arithmetic and copies ran while one was open for 4% -> 0% of each run, Pallas kernels for 0% -> 0%
where the time goes in v1:
time: 173 us
  Pallas kernels  171 us (99%)
  local copies, waits for them, and re-layouts  1.99 us (1%)
    pallas_call x1, Pallas kernels, local(): pl.pallas_call(functools.partial(kernel, n, heads), out_shape=jax.ShapeDt...  171 us

profile of v1, /device:TPU:40, one launch (start us, length us, event | category | flops | bytes accessed | tf_op | source)
XLA Modules:
  0.0 172.8 jit_solution(9777135126592445280)
XLA Ops:
  0.0 0.1 maximum_bitcast_fusion.freq_ref
  0.1 0.0 copy-start
  0.1 0.0 copy-start.1
  0.1 0.0 copy-start.2
  0.1 0.0 copy-start.3
  0.1 0.0 copy-start.4
  0.1 0.0 copy-start.5
  0.1 0.0 copy-start.6
  0.1 0.0 copy-start.7
  0.2 0.0 copy-start.8
  0.2 0.0 copy-start.9
  0.2 1.3 copy.12.tok_ref
  1.5 0.0 copy-done
  1.5 0.0 copy-done.1
  1.5 0.0 copy-done.2
  1.5 0.0 copy-done.3
  1.5 0.0 copy-done.4
  1.5 0.0 copy-done.5
  1.5 0.0 copy-done.6
  1.5 0.0 copy-done.7
  1.5 0.0 copy-done.8
  1.5 0.0 copy-done.9
  1.6 170.5 %shard_map.109 = bf16[256,256]{1,0:T(8,128)(2,1)S(1)} custom-call(f32[1,128]{1,0:T(1,128)S(1)} %maximum_bitcast_fusion.freq_ref, bf16[256,576]{1,0:T(8,128)(2,1)S(1)} %copy.12.tok_ref, bf16[144,256]{1,0:T(8,128)(2,1)S(1)} %copy-done.2, bf16[144,128]{1,0:T(8,128)(2,1)S(1)} %copy-done.3, bf16[144,128]{1,0:T(8,128)(2,1)S(1)} %copy-done.4, ...), custom_call_target="tpu_custom_call" | custom-call | tf_op jit(solution)/shard_map/pallas_call | solution.py:353
  172.1 0.7 copy.14
  (1 shorter events, 0.0 us)
Async XLA Ops:
  0.1 1.4 copy-start
  0.1 1.4 copy-start.1
  0.1 1.4 copy-start.2
  0.1 1.4 copy-start.3
  0.1 1.4 copy-start.4
  0.1 1.4 copy-start.5
  0.1 1.4 copy-start.6
  0.1 1.4 copy-start.7
  0.2 1.4 copy-start.8
  0.2 1.4 copy-start.9
